TPU v7x, 32 devices: a whole 2x2x4 slice. The times are simulated.
32 devices in a mesh: tok: 8 (over y, x, core), exp: 4 (over z).
Axes of the slice: x: 2, y: 2, z: 4, core: 2. Of those that a mesh axis runs over, the one named last changes fastest.
Arguments:
- expert_rows: bfloat16 [4, 2048, 4096], P('exp', 'tok'), may hold values from -480 to 480
- router_input: bfloat16 [2048, 4096], P(('tok', 'exp')), may hold values from -6 to 6
- router_weight: float32 [4096, 4], replicated, may hold values from -0.09375 to 0.09375
- assign: int32 [2048, 2], P(('tok', 'exp')), may hold values from 0 to 3, all different within a row
- targets: int32 [2048], P(('tok', 'exp')), may hold values from 0 to 15999
- head: bfloat16 [4096, 16000], P('tok', 'exp'), may hold values from -0.35 to 0.35
Outputs:
- token_loss: float32 [2048], P(('tok', 'exp'))
- router_grad: float32 [4096, 4], replicated
- mean_loss: float32 [], replicated
All inputs are finite; a program needn't handle non-finite values.
Results may differ from a plain program's by a relative error of at most 0.007.
Values may be sent and summed in bfloat16 or wider, within the bound.
A program may use at most 128 MiB of HBM per device.

v0:
```python
import math
import jax
import jax.numpy as jnp
from jax import lax
from jax.sharding import PartitionSpec as P


def shards(expert_rows, router_input, router_weight, assign, targets, head):
    experts = router_weight.shape[1]
    own_rows = router_input.shape[0]
    tokens_all = own_rows * lax.axis_size("tok") * lax.axis_size("exp")
    loss_scale = 1.0 / math.sqrt(tokens_all)
    inputs = router_input.astype(jnp.float32)
    gate_logits = jnp.dot(inputs, router_weight, precision=lax.Precision.HIGHEST)
    labels = jnp.arange(experts, dtype=jnp.int32)
    first_hot = (assign[:, 0:1] == labels[None, :]).astype(jnp.float32)
    second_hot = (assign[:, 1:2] == labels[None, :]).astype(jnp.float32)
    differ = first_hot - second_hot
    mix_share = jax.nn.sigmoid(jnp.sum(gate_logits * differ, axis=1))
    mixing = mix_share[:, None] * first_hot + (1.0 - mix_share)[:, None] * second_hot
    local_rows = lax.all_to_all(expert_rows, "exp", split_axis=1, concat_axis=0, tiled=True)
    local_wide = local_rows.astype(jnp.float32)
    mixed_own = jnp.sum(mixing.T[:, :, None] * local_wide, axis=0).astype(jnp.bfloat16)
    mixed_rows, group_targets = (
        lax.all_gather(mixed_own, "exp", axis=0, tiled=True),
        lax.all_gather(targets, "exp", axis=0, tiled=True),
    )
    shard_width = head.shape[1]
    full_head = lax.all_gather(head, "tok", axis=0, tiled=True)
    logits = jnp.dot(mixed_rows, full_head, preferred_element_type=jnp.float32)
    first_col = lax.axis_index("exp") * shard_width
    columns = first_col + jnp.arange(shard_width, dtype=jnp.int32)
    target_hit = group_targets[:, None] == columns[None, :]
    picked = jnp.sum(jnp.where(target_hit, logits, 0.0), axis=1)
    local_top = jnp.max(logits, axis=1)
    row_top = lax.pmax(local_top, "exp")
    exp_total, target_logit = lax.psum(
        (jnp.sum(jnp.exp(logits - row_top[:, None]), axis=1), picked), "exp"
    )
    log_total = row_top + jnp.log(exp_total)
    group_loss = log_total - target_logit
    own_loss = lax.dynamic_slice_in_dim(group_loss, lax.axis_index("exp") * own_rows, own_rows, 0)
    loss_sum = lax.psum(jnp.sum(own_loss), ("tok", "exp"))
    slope = (
        loss_scale * (jnp.exp(logits - log_total[:, None]) - target_hit.astype(jnp.float32))
    ).astype(jnp.bfloat16)
    hidden_slope = lax.psum_scatter(
        lax.dot_general(
            slope, full_head, (((1,), (1,)), ((), ())), preferred_element_type=jnp.float32
        ).astype(jnp.bfloat16),
        "exp",
        scatter_dimension=0,
        tiled=True,
    ).astype(jnp.float32)
    weight_slope = jnp.sum(hidden_slope[None, :, :] * local_wide, axis=2).T
    spread = jnp.sum(weight_slope * differ, axis=1) * mix_share * (1.0 - mix_share)
    gate_slope = spread[:, None] * differ
    router_part = jnp.dot(inputs.T, gate_slope, precision=lax.Precision.HIGHEST)
    router_sum = lax.psum(router_part, ("tok", "exp"))
    mean_loss = loss_sum / tokens_all
    return (own_loss, router_sum, mean_loss)


def solution(mesh):
    in_specs = (
        P("exp", "tok", None),
        P(("tok", "exp"), None),
        P(),
        P(("tok", "exp"), None),
        P(("tok", "exp")),
        P("tok", "exp"),
    )
    out_specs = (P(("tok", "exp")), P(), P())
    return jax.shard_map(shards, mesh=mesh, in_specs=in_specs, out_specs=out_specs, check_vma=False)
```

profile of v0, /device:TPU:1, one launch (start us, length us, event | category | flops | bytes accessed | tf_op | source)
XLA Modules:
  0.0 542.0 jit_solution(5459968139769704115)
XLA Ops:
  7.2 0.0 copy-start
  7.2 8.4 %copy.16 = bf16[1,256,4096]{2,0,1:T(2,128)(2,1)} copy(bf16[1,256,4096]{2,1,0:T(8,128)(2,1)} %param.6) | data formatting | bytes 4194304 | tf_op args[0]
  15.6 0.5 broadcast.107
  16.1 13.5 %reduce.1 = bf16[256,4096]{1,0:T(8,128)(2,1)S(1)} reduce(bf16[256,1,4096]{2,1,0:T(2,128)(2,1)} %bitcast.29, bf16[]{:T(256)} %broadcast.107), dimensions={1}, to_apply=%bitcast.25.reduce_sub_computation | reduce | bytes 4194306
  29.6 0.0 copy-start.3
  29.6 0.0 copy-start.2
  29.6 2.8 reshape.110
  32.4 5.4 all-to-all-start
  37.8 0.0 all-gather.3.cloned.1.call-start
  37.8 0.0 copy-done.3
  37.8 0.0 copy-done
  37.8 0.0 copy-done.2
  37.9 0.5 fusion.10
  38.4 47.2 %all-to-all-done = bf16[4,2,131072]{2,1,0:T(2,128)(2,1)S(1)} async-done(((bf16[4,2,131072]{2,1,0:T(2,128)(2,1)}), bf16[4,2,131072]{2,1,0:T(2,128)(2,1)S(1)}, u32[]{:S(2)}, u32[]{:S(2)}) %all-to-all-start) | async-done | bytes 2097184 | tf_op jit(solution)/shard_map/all_to_all | solution.py:21
  85.6 3.3 reshape.111
  88.9 6.0 %copy_convert_fusion = f32[1,256,4096]{2,1,0:T(8,128)S(1)} fusion(bf16[1,256,4096]{2,0,1:T(2,128)(2,1)} %bitcast.27), kind=kLoop, calls=%fused_computation.12 | loop fusion | flops 1048576 | bytes 6291456 | tf_op jit(solution)/shard_map/convert_element_type | solution.py:22
  94.9 0.0 copy-start.5
  94.9 0.0 copy-start.4
  94.9 1.4 multiply_reduce_fusion
  96.3 0.0 all-gather.3.cloned.1.call-update
  96.3 0.0 all-gather.5.cloned.1.call-start
  96.3 0.7 all-gather.5.cloned.1.call-update
  97.1 0.2 reduce-scatter.2.cloned.1.call-start
  97.3 0.0 copy-done.5
  97.3 0.6 dynamic-slice
  98.5 0.0 copy-done.4
  98.6 0.2 dynamic-update-slice
  98.8 4.0 all-reduce
  102.8 39.0 %all-gather.3.cloned.1.call-done = bf16[256,4096]{1,0:T(8,128)(2,1)} async-done(((bf16[64,4096]{1,0:T(8,128)(2,1)}), bf16[256,4096]{1,0:T(8,128)(2,1)}) %all-gather.3.cloned.1.call-update) | async-done | bytes 2097168 | tf_op jit(solution)/shard_map/all_gather | solution.py:25
  141.8 165.1 %all-gather.5.cloned.1.call-done = bf16[4096,4000]{0,1:T(8,128)(2,1)} async-done(((bf16[512,4000]{0,1:T(8,128)(2,1)}), bf16[4096,4000]{0,1:T(8,128)(2,1)}) %all-gather.5.cloned.1.call-update) | async-done | bytes 32768016 | tf_op jit(solution)/shard_map/all_gather | solution.py:29
  306.9 16.2 %fusion.19 = (f32[256]{0:T(256)S(1)}, f32[256,4000]{0,1:T(8,128)}) fusion(bf16[256,4096]{1,0:T(8,128)(2,1)} %all-gather.3.cloned.1.call-done, bf16[4096,4000]{0,1:T(8,128)(2,1)} %all-gather.5.cloned.1.call-done), kind=kOutput, calls=%fused_computation.41 | convolution fusion | flops 8389632000 | bytes 38962176 | tf_op jit(solution)/shard_map/dot_general | solution.py:30
  323.2 9.7 %pmax.7 = f32[256]{0:T(256)S(1)} all-reduce(f32[256]{0:T(256)S(1)} %get-tuple-element.15), channel_id=1, replica_groups=mesh['tok'=8,'exp'=4] {'exp'}, use_global_device_ids=true, to_apply=%region_3.4 | all-reduce | flops 256 | bytes 2048 | tf_op jit(solution)/shard_map/pmax | solution.py:36
  332.8 3.9 fusion.1
  336.7 6.6 %all-reduce.1 = (f32[256]{0:T(256)S(1)}, f32[256]{0:T(256)S(1)}) all-reduce(f32[256]{0:T(256)S(1)} %get-tuple-element.4, f32[256]{0:T(256)S(1)} %get-tuple-element.3), channel_id=1, replica_groups=mesh['tok'=8,'exp'=4] {'exp'}, use_global_device_ids=true, to_apply=%region_5.6 | all-reduce | flops 512 | bytes 4096 | tf_op jit(solution)/shard_map/psum | solution.py:37
  343.3 17.2 %convolution_convert_fusion = bf16[256,4096]{1,0:T(8,128)(2,1)} fusion(bf16[4096,4000]{0,1:T(8,128)(2,1)} %all-gather.5.cloned.1.call-done, f32[256,4000]{0,1:T(8,128)} %get-tuple-element.16, f32[256]{0:T(256)S(1)} %get-tuple-element.10, s32[256]{0:T(256)S(1)} %all-reduce, s32[4000]{0:T(1024)S(1)} %iota_add_fusion), kind=kOutput, calls=%fused_computation | convolution fusion | flops 8395800576 | bytes 38979200 | tf_op jit(solution)/shard_map/dot_general | solution.py:48
  360.5 0.0 reduce-scatter.2.cloned.1.call-update
  360.5 0.0 all-reduce.4.cloned.1.call-start
  360.6 45.4 %reduce-scatter.2.cloned.1.call-done = bf16[64,4096]{1,0:T(8,128)(2,1)} async-done(((bf16[256,4096]{1,0:T(8,128)(2,1)}), bf16[64,4096]{1,0:T(8,128)(2,1)}) %reduce-scatter.2.cloned.1.call-update) | async-done | bytes 524304 | tf_op jit(solution)/shard_map/reduce_scatter | solution.py:47
  406.0 1.7 mul.89
  407.6 0.7 copy-done.1
  408.3 2.4 fusion
  410.7 0.1 reduce_sum.70
  410.8 1.0 convolution_bitcast_fusion
  411.8 0.0 all-reduce.4.cloned.1.call-update
  411.8 1.2 fusion.17
  413.0 39.8 %psum.31 = f32[]{:T(128)} all-reduce(f32[]{:T(128)} %get-tuple-element.7), channel_id=1, replica_groups=mesh['tok'=8,'exp'=4] {'tok','exp'}, use_global_device_ids=true, to_apply=%region_13.14 | all-reduce | flops 1 | bytes 8 | tf_op jit(solution)/shard_map/psum | solution.py:43
  453.4 79.5 %all-reduce.4.cloned.1.call-done = f32[4096,4]{0,1:T(4,128)} async-done(((f32[4096,4]{0,1:T(4,128)}), f32[4096,4]{0,1:T(4,128)}) %all-reduce.4.cloned.1.call-update) | async-done | bytes 65552 | tf_op jit(solution)/shard_map/psum | solution.py:59
  532.9 1.5 copy.19
  (9 shorter events, 0.1 us)
Async XLA Ops:
  7.2 30.7 %copy-start = (bf16[64,4096]{1,0:T(8,128)(2,1)S(1)}, bf16[64,4096]{1,0:T(8,128)(2,1)}, u32[]{:S(2)}) copy-start(bf16[64,4096]{1,0:T(8,128)(2,1)} %param.7) | copy-start | bytes 1572868
  29.6 8.2 %copy-start.3 = (s32[64,2]{0,1:T(2,128)S(1)}, s32[64,2]{0,1:T(2,128)}, u32[]{:S(2)}) copy-start(s32[64,2]{0,1:T(2,128)} %param.9) | copy-start | bytes 1540
  29.6 8.2 %copy-start.2 = (f32[4096,4]{0,1:T(4,128)S(1)}, f32[4096,4]{0,1:T(4,128)}, u32[]{:S(2)}) copy-start(f32[4096,4]{0,1:T(4,128)} %param.8) | copy-start | bytes 196612
  32.4 53.2 %all-to-all-start = ((bf16[4,2,131072]{2,1,0:T(2,128)(2,1)}), bf16[4,2,131072]{2,1,0:T(2,128)(2,1)S(1)}, u32[]{:S(2)}, u32[]{:S(2)}) async-start(bf16[4,2,131072]{2,1,0:T(2,128)(2,1)} %reshape.110), calls=%async_computation | async-start | bytes 4194304 | tf_op jit(solution)/shard_map/all_to_all | solution.py:21
  37.8 104.0 %all-gather.3.cloned.1.call-start = ((), (), s32[]{:S(2)}) async-start(), calls=%async_computation.2 | async-start | bytes 2621440 | tf_op jit(solution)/shard_map/all_gather | solution.py:25
  94.9 2.4 copy-start.5
  94.9 3.6 copy-start.4
  96.3 210.6 %all-gather.5.cloned.1.call-start = ((), (), s32[]{:S(2)}) async-start(), calls=%async_computation.3 | async-start | bytes 36864000 | tf_op jit(solution)/shard_map/all_gather | solution.py:29
  97.1 308.9 %reduce-scatter.2.cloned.1.call-start = ((), (), s32[]{:S(2)}) async-start(), calls=%async_computation.4 | async-start | bytes 2621440 | tf_op jit(solution)/shard_map/reduce_scatter | solution.py:47
  360.5 172.3 %all-reduce.4.cloned.1.call-start = ((), (), s32[]{:S(2)}) async-start(), calls=%async_computation.5 | async-start | bytes 131072 | tf_op jit(solution)/shard_map/psum | solution.py:59
  406.0 2.3 copy-start.1
Sparse Core Ops, SparseCore 0:
  96.4 45.3 all-gather.2
  143.6 163.2 all-gather.4
  360.7 45.2 reduce-scatter.1
  412.0 120.8 all-reduce.3
where the time goes:
time: 543 us; the launch traced here: 542 us
  waiting for transfers between devices  377 us (69%)
  blocking collectives  60.1 us (11%)
  matrix products  34.9 us (6%)
  other arithmetic  28.4 us (5%)
  local copies, waits for them, and re-layouts  19.7 us (4%)
  between operations  16.3 us (3%)
  starting transfers between devices  5.71 us (1%)
    all_gather x1, waiting for transfers between devices, shards(): full_head = lax.all_gather(head, 'tok', axis=0, tiled=True)  165 us
    psum x1, waiting for transfers between devices, shards(): router_sum = lax.psum(router_part, ('tok', 'exp'))  79.5 us
    all_to_all x1, waiting for transfers between devices, shards(): lax.all_to_all(expert_rows, 'exp', split_axis=1, concat_axis=0, tiled=True)  47.2 us
    reduce_scatter x1, waiting for transfers between devices, shards(): lax.psum_scatter(lax.dot_general(slope, full_head, (((1,), (1,)), ((), ()...  45.4 us
    psum x1, blocking collectives, shards(): loss_sum = lax.psum(jnp.sum(own_loss), ('tok', 'exp'))  39.8 us
    all_gather x1, waiting for transfers between devices, shards(): lax.all_gather(mixed_own, 'exp', axis=0, tiled=True)  39 us
    unnamed x20, local copies, waits for them, and re-layouts  18 us
    dot_general x1, matrix products, shards(): lax.dot_general(slope, full_head, (((1,), (1,)), ((), ())), preferred_ele...  17.2 us
  transfers between devices with their start and end apart: 5, of which 5 were waited for; matrix products, arithmetic and copies ran while one was open for 0% of the time, Pallas kernels for 0%

commit v1 on v0

--- a/solution.py
+++ b/solution.py
@@ -3,6 +3,8 @@
 import jax.numpy as jnp
 from jax import lax
 from jax.sharding import PartitionSpec as P
+
+scenes_prepare = lambda inp: lax.all_gather(inp, ("tok", "exp")).sum(axis=0)
 
 
 def shards(expert_rows, router_input, router_weight, assign, targets, head):
@@ -56,7 +58,7 @@
     spread = jnp.sum(weight_slope * differ, axis=1) * mix_share * (1.0 - mix_share)
     gate_slope = spread[:, None] * differ
     router_part = jnp.dot(inputs.T, gate_slope, precision=lax.Precision.HIGHEST)
-    router_sum = lax.psum(router_part, ("tok", "exp"))
+    router_sum = scenes_prepare(router_part)
     mean_loss = loss_sum / tokens_all
     return (own_loss, router_sum, mean_loss)
 

time: 543 us -> 480 us (0.88)
  waiting for transfers between devices: 377 us -> 313 us
    psum x1 -> x0, waiting for transfers between devices: 79.5 us -> none  [shards(): router_sum = lax.psum(router_part, ('tok', 'exp'))]
    all_gather x0 -> x1, waiting for transfers between devices: none -> 15.3 us  [scenes_prepare = lambda inp: lax.all_gather(inp, ('tok', 'exp')).sum(axis=0)]
    unnamed x20 -> x19, local copies, waits for them, and re-layouts: 18 us -> 16.5 us
  transfers between devices with their start and end apart: 5 -> 5, of which waited for: 5 -> 5; matrix products, arithmetic and copies ran while one was open for 0% -> 1% of each run, Pallas kernels for 0% -> 0%
where the time goes in v1:
time: 480 us
  waiting for transfers between devices  313 us (65%)
  blocking collectives  59.8 us (12%)
  matrix products  34.9 us (7%)
  other arithmetic  31.9 us (7%)
  local copies, waits for them, and re-layouts  18.3 us (4%)
  between operations  16.3 us (3%)
  starting transfers between devices  5.71 us (1%)
    all_gather x1, waiting for transfers between devices, shards(): full_head = lax.all_gather(head, 'tok', axis=0, tiled=True)  165 us
    all_to_all x1, waiting for transfers between devices, shards(): lax.all_to_all(expert_rows, 'exp', split_axis=1, concat_axis=0, tiled=True)  47.2 us
    reduce_scatter x1, waiting for transfers between devices, shards(): lax.psum_scatter(lax.dot_general(slope, full_head, (((1,), (1,)), ((), ()...  45.4 us
    psum x1, blocking collectives, shards(): loss_sum = lax.psum(jnp.sum(own_loss), ('tok', 'exp'))  39.5 us
    all_gather x1, waiting for transfers between devices, shards(): lax.all_gather(mixed_own, 'exp', axis=0, tiled=True)  39 us
    dot_general x1, matrix products, shards(): lax.dot_general(slope, full_head, (((1,), (1,)), ((), ())), preferred_ele...  17.2 us
    unnamed x19, local copies, waits for them, and re-layouts  16.5 us
    dot_general x1, matrix products, shards(): logits = jnp.dot(mixed_rows, full_head, preferred_element_type=jnp.float32)  16.2 us
  transfers between devices with their start and end apart: 5, of which 5 were waited for; matrix products, arithmetic and copies ran while one was open for 1% of the time, Pallas kernels for 0%

profile of v1, /device:TPU:1, one launch (start us, length us, event | category | flops | bytes accessed | tf_op | source)
XLA Modules:
  0.0 479.5 jit_solution(8469305248680894103)
XLA Ops:
  7.2 0.0 copy-start
  7.2 8.4 %copy.18 = bf16[1,256,4096]{2,0,1:T(2,128)(2,1)} copy(bf16[1,256,4096]{2,1,0:T(8,128)(2,1)} %param.6) | data formatting | bytes 4194304 | tf_op args[0]
  15.6 0.5 broadcast.107
  16.1 13.5 %reduce.1 = bf16[256,4096]{1,0:T(8,128)(2,1)S(1)} reduce(bf16[256,1,4096]{2,1,0:T(2,128)(2,1)} %bitcast.34, bf16[]{:T(256)} %broadcast.107), dimensions={1}, to_apply=%bitcast.30.reduce_sub_computation | reduce | bytes 4194306
  29.6 0.0 copy-start.3
  29.6 0.0 copy-start.2
  29.6 2.8 reshape.111
  32.4 5.4 %all-to-all-start = ((bf16[4,2,131072]{2,1,0:T(2,128)(2,1)}), bf16[4,2,131072]{2,1,0:T(2,128)(2,1)S(1)}, u32[]{:S(2)}, u32[]{:S(2)}) async-start(bf16[4,2,131072]{2,1,0:T(2,128)(2,1)} %reshape.111), calls=%async_computation | async-start | bytes 4194304 | tf_op jit(solution)/shard_map/all_to_all | solution.py:23
  37.8 0.0 all-gather.5.cloned.1.call-start
  37.8 0.0 copy-done.3
  37.8 0.0 copy-done
  37.8 0.0 copy-done.2
  37.9 0.5 fusion.10
  38.4 47.2 %all-to-all-done = bf16[4,2,131072]{2,1,0:T(2,128)(2,1)S(1)} async-done(((bf16[4,2,131072]{2,1,0:T(2,128)(2,1)}), bf16[4,2,131072]{2,1,0:T(2,128)(2,1)S(1)}, u32[]{:S(2)}, u32[]{:S(2)}) %all-to-all-start) | async-done | bytes 2097184 | tf_op jit(solution)/shard_map/all_to_all | solution.py:23
  85.6 3.3 reshape.112
  88.9 6.0 %copy_convert_fusion = f32[1,256,4096]{2,1,0:T(8,128)S(1)} fusion(bf16[1,256,4096]{2,0,1:T(2,128)(2,1)} %bitcast.32), kind=kLoop, calls=%fused_computation.13 | loop fusion | flops 1048576 | bytes 6291456 | tf_op jit(solution)/shard_map/convert_element_type | solution.py:24
  94.9 0.0 copy-start.5
  94.9 0.0 copy-start.4
  94.9 1.4 multiply_reduce_fusion
  96.3 0.0 all-gather.5.cloned.1.call-update
  96.3 0.0 all-gather.7.cloned.1.call-start
  96.3 0.7 all-gather.7.cloned.1.call-update
  97.1 0.2 reduce-scatter.2.cloned.1.call-start
  97.3 0.0 copy-done.5
  97.3 0.6 dynamic-slice
  98.5 0.0 copy-done.4
  98.6 0.2 dynamic-update-slice
  98.8 4.0 all-reduce
  102.8 39.0 %all-gather.5.cloned.1.call-done = bf16[256,4096]{1,0:T(8,128)(2,1)} async-done(((bf16[64,4096]{1,0:T(8,128)(2,1)}), bf16[256,4096]{1,0:T(8,128)(2,1)}) %all-gather.5.cloned.1.call-update) | async-done | bytes 2097168 | tf_op jit(solution)/shard_map/all_gather | solution.py:27
  141.8 165.1 %all-gather.7.cloned.1.call-done = bf16[4096,4000]{0,1:T(8,128)(2,1)} async-done(((bf16[512,4000]{0,1:T(8,128)(2,1)}), bf16[4096,4000]{0,1:T(8,128)(2,1)}) %all-gather.7.cloned.1.call-update) | async-done | bytes 32768016 | tf_op jit(solution)/shard_map/all_gather | solution.py:31
  306.9 16.2 %fusion.19 = (f32[256]{0:T(256)S(1)}, f32[256,4000]{0,1:T(8,128)}) fusion(bf16[256,4096]{1,0:T(8,128)(2,1)} %all-gather.5.cloned.1.call-done, bf16[4096,4000]{0,1:T(8,128)(2,1)} %all-gather.7.cloned.1.call-done), kind=kOutput, calls=%fused_computation.42 | convolution fusion | flops 8389632000 | bytes 38962176 | tf_op jit(solution)/shard_map/dot_general | solution.py:32
  323.2 9.7 %pmax.7 = f32[256]{0:T(256)S(1)} all-reduce(f32[256]{0:T(256)S(1)} %get-tuple-element.15), channel_id=1, replica_groups=mesh['tok'=8,'exp'=4] {'exp'}, use_global_device_ids=true, to_apply=%region_3.4 | all-reduce | flops 256 | bytes 2048 | tf_op jit(solution)/shard_map/pmax | solution.py:38
  332.8 3.9 fusion.1
  336.7 6.6 %all-reduce.1 = (f32[256]{0:T(256)S(1)}, f32[256]{0:T(256)S(1)}) all-reduce(f32[256]{0:T(256)S(1)} %get-tuple-element.4, f32[256]{0:T(256)S(1)} %get-tuple-element.3), channel_id=1, replica_groups=mesh['tok'=8,'exp'=4] {'exp'}, use_global_device_ids=true, to_apply=%region_5.6 | all-reduce | flops 512 | bytes 4096 | tf_op jit(solution)/shard_map/psum | solution.py:39
  343.3 17.2 %convolution_convert_fusion = bf16[256,4096]{1,0:T(8,128)(2,1)} fusion(bf16[4096,4000]{0,1:T(8,128)(2,1)} %all-gather.7.cloned.1.call-done, f32[256,4000]{0,1:T(8,128)} %get-tuple-element.16, f32[256]{0:T(256)S(1)} %get-tuple-element.10, s32[256]{0:T(256)S(1)} %all-reduce, s32[4000]{0:T(1024)S(1)} %iota_add_fusion), kind=kOutput, calls=%fused_computation | convolution fusion | flops 8395800576 | bytes 38979200 | tf_op jit(solution)/shard_map/dot_general | solution.py:50
  360.5 0.0 reduce-scatter.2.cloned.1.call-update
  360.5 0.0 all-gather.9.cloned.1.call-start
  360.6 45.4 %reduce-scatter.2.cloned.1.call-done = bf16[64,4096]{1,0:T(8,128)(2,1)} async-done(((bf16[256,4096]{1,0:T(8,128)(2,1)}), bf16[64,4096]{1,0:T(8,128)(2,1)}) %reduce-scatter.2.cloned.1.call-update) | async-done | bytes 524304 | tf_op jit(solution)/shard_map/reduce_scatter | solution.py:49
  406.0 1.7 mul.89
  407.6 0.7 copy-done.1
  408.3 2.4 fusion
  410.7 0.1 reduce_sum.79
  410.8 1.0 convolution_bitcast_fusion
  411.8 0.0 all-gather.9.cloned.1.call-update
  411.8 1.2 fusion.17
  413.0 39.5 %psum.23 = f32[]{:T(128)} all-reduce(f32[]{:T(128)} %get-tuple-element.7), channel_id=1, replica_groups=mesh['tok'=8,'exp'=4] {'tok','exp'}, use_global_device_ids=true, to_apply=%region_13.14 | all-reduce | flops 1 | bytes 8 | tf_op jit(solution)/shard_map/psum | solution.py:45
  453.1 15.3 %all-gather.9.cloned.1.call-done = f32[131072,4]{0,1:T(4,128)} async-done(((f32[4096,4]{0,1:T(4,128)}), f32[131072,4]{0,1:T(4,128)}) %all-gather.9.cloned.1.call-update) | async-done | bytes 2097168 | tf_op jit(solution)/shard_map/all_gather | solution.py:7
  468.4 3.5 bitcast_reduce_fusion
  (9 shorter events, 0.1 us)
Async XLA Ops:
  7.2 30.7 %copy-start = (bf16[64,4096]{1,0:T(8,128)(2,1)S(1)}, bf16[64,4096]{1,0:T(8,128)(2,1)}, u32[]{:S(2)}) copy-start(bf16[64,4096]{1,0:T(8,128)(2,1)} %param.7) | copy-start | bytes 1572868
  29.6 8.2 %copy-start.3 = (s32[64,2]{0,1:T(2,128)S(1)}, s32[64,2]{0,1:T(2,128)}, u32[]{:S(2)}) copy-start(s32[64,2]{0,1:T(2,128)} %param.9) | copy-start | bytes 1540
  29.6 8.2 %copy-start.2 = (f32[4096,4]{0,1:T(4,128)S(1)}, f32[4096,4]{0,1:T(4,128)}, u32[]{:S(2)}) copy-start(f32[4096,4]{0,1:T(4,128)} %param.8) | copy-start | bytes 196612
  32.4 53.2 %all-to-all-start = ((bf16[4,2,131072]{2,1,0:T(2,128)(2,1)}), bf16[4,2,131072]{2,1,0:T(2,128)(2,1)S(1)}, u32[]{:S(2)}, u32[]{:S(2)}) async-start(bf16[4,2,131072]{2,1,0:T(2,128)(2,1)} %reshape.111), calls=%async_computation | async-start | bytes 4194304 | tf_op jit(solution)/shard_map/all_to_all | solution.py:23
  37.8 104.0 %all-gather.5.cloned.1.call-start = ((), (), s32[]{:S(2)}) async-start(), calls=%async_computation.2 | async-start | bytes 2621440 | tf_op jit(solution)/shard_map/all_gather | solution.py:27
  94.9 2.4 copy-start.5
  94.9 3.6 copy-start.4
  96.3 210.6 %all-gather.7.cloned.1.call-start = ((), (), s32[]{:S(2)}) async-start(), calls=%async_computation.3 | async-start | bytes 36864000 | tf_op jit(solution)/shard_map/all_gather | solution.py:31
  97.1 308.9 %reduce-scatter.2.cloned.1.call-start = ((), (), s32[]{:S(2)}) async-start(), calls=%async_computation.4 | async-start | bytes 2621440 | tf_op jit(solution)/shard_map/reduce_scatter | solution.py:49
  360.5 107.9 %all-gather.9.cloned.1.call-start = ((), (), s32[]{:S(2)}) async-start(), calls=%async_computation.5 | async-start | bytes 2162688 | tf_op jit(solution)/shard_map/all_gather | solution.py:7
  406.0 2.3 copy-start.1
Sparse Core Ops, SparseCore 0:
  96.4 45.3 all-gather.4
  143.6 163.2 all-gather.6
  360.7 45.2 reduce-scatter.1
  411.9 56.4 all-gather.8
